TPU v7x, 32 devices: a whole 2x2x4 slice. The times are simulated.
32 devices in a mesh: rep: 2 (over x), fsdp: 4 (over y, core), seq: 4 (over z).
Axes of the slice: x: 2, y: 2, z: 4, core: 2. Of those that a mesh axis runs over, the one named last changes fastest.
Arguments:
- tokens: bfloat16 [16, 1024, 1152], P(('rep', 'fsdp'), 'seq'), may hold values from -6 to 6
- condition: bfloat16 [16, 1152], P(('rep', 'fsdp')), may hold values from -6 to 6
- valid_mask: int32 [16, 1024], P(('rep', 'fsdp'), 'seq'), may hold values from 0 to 1, as said below
- teacher: bfloat16 [16, 1024, 1152], P(('rep', 'fsdp'), 'seq'), may hold values from -6 to 6
- out_grad: bfloat16 [16, 1024, 1152], P(('rep', 'fsdp'), 'seq'), may hold values from -96 to 96
- mod_weight: bfloat16 [1152, 6912], P('fsdp'), may hold values from -0.1875 to 0.1875
- mod_bias: bfloat16 [6912], P('fsdp'), may hold values from -3 to 3
- qkv_weight: bfloat16 [1152, 3456], P('fsdp'), may hold values from -0.1875 to 0.1875
- qkv_bias: bfloat16 [2304], P('fsdp'), may hold values from -3 to 3
- out_weight: bfloat16 [1152, 1152], P('fsdp'), may hold values from -2 to 2
- out_bias: bfloat16 [1152], P('fsdp'), may hold values from -3 to 3
- up_weight: bfloat16 [1152, 4608], P('fsdp'), may hold values from -0.1875 to 0.1875
- up_bias: bfloat16 [4608], P('fsdp'), may hold values from -3 to 3
- down_weight: bfloat16 [4608, 1152], P('fsdp'), may hold values from -0.09375 to 0.09375
- down_bias: bfloat16 [1152], P('fsdp'), may hold values from -3 to 3
Outputs:
- block_out: bfloat16 [16, 1024, 1152], P(('rep', 'fsdp'), 'seq')
- loss_value: float32 [], replicated
- tokens_grad: bfloat16 [16, 1024, 1152], P(('rep', 'fsdp'), 'seq')
- condition_grad: float32 [16, 1152], P(('rep', 'fsdp'))
- mod_weight_grad: float32 [1152, 6912], P('fsdp')
- mod_bias_grad: float32 [6912], P('fsdp')
- qkv_weight_grad: float32 [1152, 3456], P('fsdp')
- qkv_bias_grad: float32 [2304], P('fsdp')
- out_weight_grad: float32 [1152, 1152], P('fsdp')
- out_bias_grad: float32 [1152], P('fsdp')
- up_weight_grad: float32 [1152, 4608], P('fsdp')
- up_bias_grad: float32 [4608], P('fsdp')
- down_weight_grad: float32 [4608, 1152], P('fsdp')
- down_bias_grad: float32 [1152], P('fsdp')
Inputs may be any that keep to these rules, and one draw needn't show every extreme that they name: `valid_mask`: the first token of every latent is valid.
All inputs are finite; a program needn't handle non-finite values.
Results may differ from a plain program's by a relative error of at most 0.012.
Values may be sent and summed in bfloat16 or wider, within the bound.
A program may use at most 256 MiB of HBM per device.

v0:
```python
import jax
import jax.numpy as jnp
from jax import lax
from jax.sharding import PartitionSpec as P

HEADS = 16
EPS = 1e-06
GELU_C = 0.7978845608028654
HIGHEST = lax.Precision.HIGHEST


def norm_rows(inputs):
    centred = inputs - jnp.mean(inputs, axis=-1, keepdims=True)
    return centred * lax.rsqrt(jnp.mean(centred * centred, axis=-1, keepdims=True) + EPS)


def gelu_tanh(inputs):
    return 0.5 * inputs * (1.0 + jnp.tanh(GELU_C * (inputs + 0.044715 * inputs * inputs * inputs)))


def modulate(inputs, offset, stretch):
    return norm_rows(inputs) * (1.0 + stretch) + offset


def flat_dot(left, right):
    return jnp.dot(left.reshape(-1, left.shape[-1]), right, preferred_element_type=jnp.float32)


def flat_dot_t(left, right):
    return lax.dot_general(
        left.reshape(-1, left.shape[-1]),
        right,
        (((1,), (1,)), ((), ())),
        preferred_element_type=jnp.float32,
    )


def outer_sum(left, right):
    return lax.dot_general(
        left.reshape(-1, left.shape[-1]),
        right.reshape(-1, right.shape[-1]),
        (((0,), (0,)), ((), ())),
        preferred_element_type=jnp.float32,
    )


def outer_exact(left, right):
    return lax.dot_general(
        left, right, (((0,), (0,)), ((), ())), precision=HIGHEST, preferred_element_type=jnp.float32
    )


def shards(
    tokens,
    condition,
    valid_mask,
    teacher,
    out_grad,
    mod_weight,
    mod_bias,
    qkv_weight,
    qkv_bias,
    out_weight,
    out_bias,
    up_weight,
    up_bias,
    down_weight,
    down_bias,
):
    gathered = (
        lax.all_gather(mod_weight, "fsdp", axis=0, tiled=True),
        lax.all_gather(mod_bias, "fsdp", axis=0, tiled=True),
        lax.all_gather(qkv_weight, "fsdp", axis=0, tiled=True),
        lax.all_gather(qkv_bias, "fsdp", axis=0, tiled=True),
        lax.all_gather(out_weight, "fsdp", axis=0, tiled=True),
        lax.all_gather(out_bias, "fsdp", axis=0, tiled=True),
        lax.all_gather(up_weight, "fsdp", axis=0, tiled=True),
        lax.all_gather(up_bias, "fsdp", axis=0, tiled=True),
        lax.all_gather(down_weight, "fsdp", axis=0, tiled=True),
        lax.all_gather(down_bias, "fsdp", axis=0, tiled=True),
    )
    (
        mod_full,
        modb_full,
        qkv_full,
        qkvb_full,
        out_full,
        outb_full,
        up_full,
        upb_full,
        down_full,
        downb_full,
    ) = gathered
    latents, rows, width = tokens.shape
    head_dim = width // HEADS
    factor = head_dim ** (-0.5)
    total_tokens = (
        latents * rows * lax.axis_size("rep") * lax.axis_size("fsdp") * lax.axis_size("seq")
    )
    keyvalid = valid_mask.astype(jnp.float32)
    counted = lax.psum(jnp.sum(keyvalid), ("rep", "fsdp", "seq"))
    inputs = tokens.astype(jnp.float32)
    conds = condition.astype(jnp.float32)
    silu_low = jax.nn.silu(conds).astype(jnp.bfloat16)
    modulation = jnp.dot(silu_low, mod_full, preferred_element_type=jnp.float32) + modb_full.astype(
        jnp.float32
    )
    pieces = [modulation[:, None, number * width : (number + 1) * width] for number in range(6)]
    shift_one, scale_one, gate_one, shift_two, scale_two, gate_two = pieces
    hidden_one = modulate(inputs, shift_one, scale_one).astype(jnp.bfloat16)
    projected = flat_dot(hidden_one, qkv_full).reshape(latents, rows, 3 * width)
    qkv_bias_f = qkvb_full.astype(jnp.float32)
    queries = (projected[..., :width] + qkv_bias_f[:width]).astype(jnp.bfloat16)
    keys_own = projected[..., width : 2 * width].astype(jnp.bfloat16)
    values_own = (projected[..., 2 * width :] + qkv_bias_f[width:]).astype(jnp.bfloat16)
    all_keys, all_values, all_valid = (
        lax.all_gather(keys_own, "seq", axis=1, tiled=True),
        lax.all_gather(values_own, "seq", axis=1, tiled=True),
        lax.all_gather(keyvalid.astype(jnp.bfloat16), "seq", axis=1, tiled=True),
    )
    keep_mask = (all_valid > 0.5)[:, None, :]

    def split_heads(tensor):
        return tensor.reshape(latents, tensor.shape[1], HEADS, head_dim).transpose(2, 0, 1, 3)

    def merge_heads(tensor):
        return tensor.transpose(1, 2, 0, 3).reshape(latents, tensor.shape[2], width)

    def scores_of(q_head, k_head, mask):
        scores = (
            jnp.einsum("gqd,gkd->gqk", q_head, k_head, preferred_element_type=jnp.float32) * factor
        )
        return jnp.where(mask, scores, -1e30)

    def head_forward(packed):
        q_head, k_head, v_head = packed
        scores = scores_of(q_head, k_head, keep_mask)
        maxima = jnp.max(scores, axis=-1, keepdims=True)
        expsum = jnp.exp(scores - maxima)
        totals = jnp.sum(expsum, axis=-1, keepdims=True)
        probability = (expsum / totals).astype(jnp.bfloat16)
        mixture = jnp.einsum(
            "gqk,gkd->gqd", probability, v_head, preferred_element_type=jnp.float32
        )
        return (mixture, (maxima + jnp.log(totals))[..., 0])

    q_heads = split_heads(queries)
    k_heads = split_heads(all_keys)
    v_heads = split_heads(all_values)
    mixed_heads, logsum = lax.map(head_forward, (q_heads, k_heads, v_heads))
    attended = merge_heads(mixed_heads).astype(jnp.bfloat16)
    branch = flat_dot(attended, out_full).reshape(latents, rows, width) + outb_full.astype(
        jnp.float32
    )
    middle = inputs + gate_one * branch
    hidden_two = modulate(middle, shift_two, scale_two).astype(jnp.bfloat16)
    up_pre = flat_dot(hidden_two, up_full) + upb_full.astype(jnp.float32)
    activated = gelu_tanh(up_pre).astype(jnp.bfloat16)
    mlp_out = (flat_dot(activated, down_full) + downb_full.astype(jnp.float32)).reshape(
        latents, rows, width
    )
    output = middle + gate_two * mlp_out
    differ = output - teacher.astype(jnp.float32)
    err_sum = jnp.sum(keyvalid[..., None] * differ * differ)
    regathered = (
        lax.all_gather(mod_weight, "fsdp", axis=0, tiled=True),
        lax.all_gather(mod_bias, "fsdp", axis=0, tiled=True),
        lax.all_gather(qkv_weight, "fsdp", axis=0, tiled=True),
        lax.all_gather(qkv_bias, "fsdp", axis=0, tiled=True),
        lax.all_gather(out_weight, "fsdp", axis=0, tiled=True),
        lax.all_gather(out_bias, "fsdp", axis=0, tiled=True),
        lax.all_gather(up_weight, "fsdp", axis=0, tiled=True),
        lax.all_gather(up_bias, "fsdp", axis=0, tiled=True),
        lax.all_gather(down_weight, "fsdp", axis=0, tiled=True),
        lax.all_gather(down_bias, "fsdp", axis=0, tiled=True),
    )
    mod_back = regathered[0]
    qkv_back = regathered[2]
    out_back = regathered[4]
    up_back = regathered[6]
    down_back = regathered[8]
    grad_out = out_grad.astype(jnp.float32) + total_tokens / counted * differ * keyvalid[..., None]
    grad_mlp = (grad_out * gate_two).astype(jnp.bfloat16)
    gate_two_grad = jnp.sum(grad_out * mlp_out, axis=1)
    down_wgrad = outer_sum(activated, grad_mlp)
    down_bgrad = jnp.sum(grad_mlp.astype(jnp.float32), axis=(0, 1))
    act_grad = flat_dot_t(grad_mlp, down_back)
    up_pre_grad = jax.vjp(gelu_tanh, up_pre)[1](act_grad)[0].astype(jnp.bfloat16)
    up_wgrad = outer_sum(hidden_two, up_pre_grad)
    up_bgrad = jnp.sum(up_pre_grad.astype(jnp.float32), axis=0)
    hidden_two_grad = flat_dot_t(up_pre_grad, up_back).reshape(latents, rows, width)
    pull_two = jax.vjp(modulate, middle, shift_two, scale_two)[1]
    middle_part, shift_two_grad, scale_two_grad = pull_two(hidden_two_grad)
    middle_grad = middle_part + grad_out
    branch_grad = (middle_grad * gate_one).astype(jnp.bfloat16)
    gate_one_grad = jnp.sum(middle_grad * branch, axis=1)
    out_wgrad = outer_sum(attended, branch_grad)
    out_bgrad = jnp.sum(branch_grad.astype(jnp.float32), axis=(0, 1))
    attended_grad = (
        flat_dot_t(branch_grad, out_back).astype(jnp.bfloat16).reshape(latents, rows, width)
    )
    dout_heads = split_heads(attended_grad)

    def head_backward(packed):
        q_head, k_head, v_head, lse_head, dout_head = packed
        scores = scores_of(q_head, k_head, keep_mask)
        probability = jnp.exp(scores - lse_head[..., None])
        value_part = jnp.einsum(
            "gqk,gqd->gkd",
            probability.astype(jnp.bfloat16),
            dout_head,
            preferred_element_type=jnp.float32,
        )
        prob_grad = jnp.einsum(
            "gqd,gkd->gqk", dout_head, v_head, preferred_element_type=jnp.float32
        )
        score_grad = (
            probability * (prob_grad - jnp.sum(probability * prob_grad, axis=-1, keepdims=True))
        ).astype(jnp.bfloat16)
        query_part = (
            jnp.einsum("gqk,gkd->gqd", score_grad, k_head, preferred_element_type=jnp.float32)
            * factor
        )
        key_part = (
            jnp.einsum("gqk,gqd->gkd", score_grad, q_head, preferred_element_type=jnp.float32)
            * factor
        )
        return (query_part, key_part, value_part)

    q_grads, k_grads, v_grads = lax.map(
        head_backward, (q_heads, k_heads, v_heads, logsum, dout_heads)
    )
    key_sum, value_sum = (
        lax.psum_scatter(merge_heads(k_grads), "seq", scatter_dimension=1, tiled=True),
        lax.psum_scatter(merge_heads(v_grads), "seq", scatter_dimension=1, tiled=True),
    )
    query_grad = merge_heads(q_grads).astype(jnp.bfloat16)
    value_grad = value_sum.astype(jnp.bfloat16)
    qkv_grad = jnp.concatenate([query_grad, key_sum.astype(jnp.bfloat16), value_grad], axis=-1)
    qkv_wgrad = outer_sum(hidden_one, qkv_grad)
    qkv_bgrad = jnp.concatenate(
        [
            jnp.sum(query_grad.astype(jnp.float32), axis=(0, 1)),
            jnp.sum(value_grad.astype(jnp.float32), axis=(0, 1)),
        ]
    )
    hidden_one_grad = flat_dot_t(qkv_grad, qkv_back).reshape(latents, rows, width)
    pull_one = jax.vjp(modulate, inputs, shift_one, scale_one)[1]
    input_part, shift_one_grad, scale_one_grad = pull_one(hidden_one_grad)
    tokens_grad = (input_part + middle_grad).astype(jnp.bfloat16)
    mod_grad = jnp.concatenate(
        [
            shift_one_grad[:, 0],
            scale_one_grad[:, 0],
            gate_one_grad,
            shift_two_grad[:, 0],
            scale_two_grad[:, 0],
            gate_two_grad,
        ],
        axis=-1,
    )
    cond_total = lax.psum(mod_grad.astype(jnp.bfloat16), "seq").astype(jnp.float32)
    silu_grad = jnp.einsum(
        "le,de->ld", cond_total, mod_back, precision=HIGHEST, preferred_element_type=jnp.float32
    )
    condition_grad = jax.vjp(jax.nn.silu, conds)[1](silu_grad)[0]
    silu_exact = silu_low.astype(jnp.float32)
    mod_term = outer_exact(silu_exact, mod_grad)
    modb_term = jnp.sum(mod_grad, axis=0)
    (
        owned_modw,
        owned_modb,
        owned_qkvw,
        owned_qkvb,
        owned_outw,
        owned_outb,
        owned_upw,
        owned_upb,
        owned_downw,
        owned_downb,
    ) = (
        lax.psum_scatter(
            mod_term.astype(jnp.bfloat16), "fsdp", scatter_dimension=0, tiled=True
        ).astype(jnp.float32),
        lax.psum_scatter(
            modb_term.astype(jnp.bfloat16), "fsdp", scatter_dimension=0, tiled=True
        ).astype(jnp.float32),
        lax.psum_scatter(
            qkv_wgrad.astype(jnp.bfloat16), "fsdp", scatter_dimension=0, tiled=True
        ).astype(jnp.float32),
        lax.psum_scatter(
            qkv_bgrad.astype(jnp.bfloat16), "fsdp", scatter_dimension=0, tiled=True
        ).astype(jnp.float32),
        lax.psum_scatter(
            out_wgrad.astype(jnp.bfloat16), "fsdp", scatter_dimension=0, tiled=True
        ).astype(jnp.float32),
        lax.psum_scatter(
            out_bgrad.astype(jnp.bfloat16), "fsdp", scatter_dimension=0, tiled=True
        ).astype(jnp.float32),
        lax.psum_scatter(
            up_wgrad.astype(jnp.bfloat16), "fsdp", scatter_dimension=0, tiled=True
        ).astype(jnp.float32),
        lax.psum_scatter(
            up_bgrad.astype(jnp.bfloat16), "fsdp", scatter_dimension=0, tiled=True
        ).astype(jnp.float32),
        lax.psum_scatter(
            down_wgrad.astype(jnp.bfloat16), "fsdp", scatter_dimension=0, tiled=True
        ).astype(jnp.float32),
        lax.psum_scatter(
            down_bgrad.astype(jnp.bfloat16), "fsdp", scatter_dimension=0, tiled=True
        ).astype(jnp.float32),
    )
    summed = (
        lax.psum(owned_modw.astype(jnp.bfloat16), ("rep", "seq")).astype(jnp.float32),
        lax.psum(owned_modb.astype(jnp.bfloat16), ("rep", "seq")).astype(jnp.float32),
        lax.psum(owned_qkvw.astype(jnp.bfloat16), ("rep", "seq")).astype(jnp.float32),
        lax.psum(owned_qkvb.astype(jnp.bfloat16), ("rep", "seq")).astype(jnp.float32),
        lax.psum(owned_outw.astype(jnp.bfloat16), ("rep", "seq")).astype(jnp.float32),
        lax.psum(owned_outb.astype(jnp.bfloat16), ("rep", "seq")).astype(jnp.float32),
        lax.psum(owned_upw.astype(jnp.bfloat16), ("rep", "seq")).astype(jnp.float32),
        lax.psum(owned_upb.astype(jnp.bfloat16), ("rep", "seq")).astype(jnp.float32),
        lax.psum(owned_downw.astype(jnp.bfloat16), ("rep", "seq")).astype(jnp.float32),
        lax.psum(owned_downb.astype(jnp.bfloat16), ("rep", "seq")).astype(jnp.float32),
    )
    err_total = lax.psum(err_sum, ("rep", "fsdp", "seq"))
    loss_value = err_total / (width * counted)
    return (
        output.astype(jnp.bfloat16),
        loss_value,
        tokens_grad,
        condition_grad,
        summed[0],
        summed[1],
        summed[2],
        summed[3],
        summed[4],
        summed[5],
        summed[6],
        summed[7],
        summed[8],
        summed[9],
    )


def solution(mesh):
    placed = (
        P(("rep", "fsdp"), "seq", None),
        P(("rep", "fsdp"), None),
        P(("rep", "fsdp"), "seq"),
        P(("rep", "fsdp"), "seq", None),
        P(("rep", "fsdp"), "seq", None),
        P("fsdp", None),
        P("fsdp"),
        P("fsdp", None),
        P("fsdp"),
        P("fsdp", None),
        P("fsdp"),
        P("fsdp", None),
        P("fsdp"),
        P("fsdp", None),
        P("fsdp"),
    )
    return jax.shard_map(
        shards,
        mesh=mesh,
        in_specs=placed,
        out_specs=(
            P(("rep", "fsdp"), "seq", None),
            P(),
            P(("rep", "fsdp"), "seq", None),
            P(("rep", "fsdp"), None),
            P("fsdp", None),
            P("fsdp"),
            P("fsdp", None),
            P("fsdp"),
            P("fsdp", None),
            P("fsdp"),
            P("fsdp", None),
            P("fsdp"),
            P("fsdp", None),
            P("fsdp"),
        ),
        check_vma=False,
    )
```

profile of v0, /device:TPU:0, one launch (start us, length us, event | category | flops | bytes accessed | tf_op | source)
XLA Modules:
  0.0 1927.1 jit_solution(1183738872839530191)
XLA Ops:
  12.4 12.9 all-reduce.13
  26.7 86.8 %all-gather.9.cloned.1.call-done = bf16[1152,6912]{1,0:T(8,128)(2,1)} async-done(((bf16[288,6912]{1,0:T(8,128)(2,1)}), bf16[1152,6912]{1,0:T(8,128)(2,1)}) %all-gather.9.cloned.1.call-update) | async-done | bytes 15925264 | tf_op jit(solution)/shard_map/all_gather | solution.py:71
  121.8 49.1 %all-gather.11.cloned.1.call-done = bf16[1152,3456]{1,0:T(8,128)(2,1)} async-done(((bf16[288,3456]{1,0:T(8,128)(2,1)}), bf16[1152,3456]{1,0:T(8,128)(2,1)}) %all-gather.11.cloned.1.call-update) | async-done | bytes 7962640 | tf_op jit(solution)/shard_map/all_gather | solution.py:73
  188.1 11.4 all_gather.46
  208.5 63.0 %all-gather.15.cloned.1.call-done = bf16[2,1024,1152]{2,1,0:T(8,128)(2,1)} async-done(((bf16[2,256,1152]{2,1,0:T(8,128)(2,1)}), bf16[2,1024,1152]{2,1,0:T(8,128)(2,1)}) %all-gather.15.cloned.1.call-update) | async-done | bytes 4718608 | tf_op jit(solution)/shard_map/all_gather | solution.py:118
  284.0 77.4 %all-gather.13.cloned.1.call-done = bf16[2,1024,1152]{2,1,0:T(8,128)(2,1)} async-done(((bf16[2,256,1152]{2,1,0:T(8,128)(2,1)}), bf16[2,1024,1152]{2,1,0:T(8,128)(2,1)}) %all-gather.13.cloned.1.call-update) | async-done | bytes 4718608 | tf_op jit(solution)/shard_map/all_gather | solution.py:117
  373.8 71.5 %while.26 = (s32[]{:T(128)}, bf16[16,2,256,72]{2,3,0,1:T(8,128)(2,1)S(1)}, f32[16,2,256]{2,1,0:T(2,128)}, pred[2,1,1024]{2,0,1:T(4,128)(4,1)S(1)}, bf16[16,2,256...) while((s32[]{:T(128)}, ...), condition=%wide.region_5.6_spmd, body=%wide.region_2.5_spmd.sunk | while | flops 157285888 | bytes 7129185 | solution.py:150
  459.3 12.8 fusion.96
  472.1 59.7 %all-gather.21.cloned.1.call-done = bf16[4608,1152]{1,0:T(8,128)(2,1)} async-done(((bf16[1152,1152]{1,0:T(8,128)(2,1)}), bf16[4608,1152]{1,0:T(8,128)(2,1)}) %all-gather.21.cloned.1.call-update) | async-done | bytes 10616848 | tf_op jit(solution)/shard_map/all_gather | solution.py:79
  531.8 13.2 convolution_add_fusion.1
  547.8 39.5 %all-reduce.9 = (f32[]{:T(128)}, f32[]{:T(128)}) all-reduce(f32[]{:T(128)} %get-tuple-element.233, f32[]{:T(128)} %convert_reduce_fusion.2), channel_id=1, replica_groups=mesh['rep'=2,'fsdp'=4,'seq'=4] {'rep','fsdp','seq'}, use_global_device_ids=true, to_apply=%region_9.10 | all-reduce | flops 2 | bytes 16 | tf_op jit(solution)/shard_map/psum | solution.py:325
  591.4 18.8 fusion.87
  630.5 142.3 %while.27 = (s32[]{:T(128)}, bf16[16,2,256,72]{2,3,0,1:T(8,128)(2,1)S(1)}, f32[16,2,1024,72]{2,3,0,1:T(8,128)}, f32[16,2,1024,72]{2,3,0,1:T(8,128)}, pred[2,1,10...) while((s32[]{:T(128)}, ...), condition=%wide.region_16.17_spmd, body=%wide.region_14.16_spmd.sunk | while | flops 382389760 | bytes 18398340 | solution.py:230
  799.1 13.0 convolution_convert_fusion.1
  824.6 120.6 %reduce-scatter.8.cloned.1.call-done = f32[2,256,1152]{2,1,0:T(8,128)} async-done(((f32[2,1024,1152]{2,1,0:T(8,128)}), f32[2,256,1152]{2,1,0:T(8,128)}) %reduce-scatter.8.cloned.1.call-update) | async-done | bytes 2359312 | tf_op jit(solution)/shard_map/reduce_scatter | solution.py:234
  947.1 162.7 %reduce-scatter.10.cloned.1.call-done = f32[2,256,1152]{2,1,0:T(8,128)} async-done(((f32[2,1024,1152]{2,1,0:T(8,128)}), f32[2,256,1152]{2,1,0:T(8,128)}) %reduce-scatter.10.cloned.1.call-update) | async-done | bytes 2359312 | tf_op jit(solution)/shard_map/reduce_scatter | solution.py:235
  1138.5 15.5 convolution_convert_fusion
  1154.1 82.3 %reduce-scatter.20.cloned.1.call-done = bf16[1152,1152]{1,0:T(8,128)(2,1)} async-done(((bf16[4608,1152]{1,0:T(8,128)(2,1)}), bf16[1152,1152]{1,0:T(8,128)(2,1)}) %reduce-scatter.20.cloned.1.call-update) | async-done | bytes 2654224 | tf_op jit(solution)/shard_map/reduce_scatter | solution.py:306
  1236.3 87.7 %reduce-scatter.18.cloned.1.call-done = bf16[288,4608]{1,0:T(8,128)(2,1)} async-done(((bf16[1152,4608]{1,0:T(8,128)(2,1)}), bf16[288,4608]{1,0:T(8,128)(2,1)}) %reduce-scatter.18.cloned.1.call-update) | async-done | bytes 2654224 | tf_op jit(solution)/shard_map/reduce_scatter | solution.py:300
  1324.1 72.1 %reduce-scatter.14.cloned.1.call-done = bf16[288,3456]{1,0:T(8,128)(2,1)} async-done(((bf16[1152,3456]{1,0:T(8,128)(2,1)}), bf16[288,3456]{1,0:T(8,128)(2,1)}) %reduce-scatter.14.cloned.1.call-update) | async-done | bytes 1990672 | tf_op jit(solution)/shard_map/reduce_scatter | solution.py:288
  1396.1 122.6 %reduce-scatter.12.cloned.1.call-done = bf16[288,6912]{1,0:T(8,128)(2,1)} async-done(((bf16[1152,6912]{1,0:T(8,128)(2,1)}), bf16[288,6912]{1,0:T(8,128)(2,1)}) %reduce-scatter.12.cloned.1.call-update) | async-done | bytes 3981328 | tf_op jit(solution)/shard_map/reduce_scatter | solution.py:282
  1537.8 39.9 %all-reduce.10 = (bf16[1728]{0:T(1024)(128)(2,1)S(1)}, bf16[576]{0:T(1024)(128)(2,1)S(1)}, bf16[288]{0:T(512)(128)(2,1)S(1)}, bf16[1152]{0:T(1024)(128)(2,1)S(1)}, bf16[288]{0:T(512)(128)(2,1)S(1)}) all-reduce(bf16[1728]{0:T(1024)(128)(2,1)S(1)} %dynamic-slice.5, ...), channel_id=1, replica_groups=mesh['rep'=2,'fsdp'=4,'seq'=4] {'rep','seq'}, use_global_device_ids=true, to_apply=%region_32.33 | all-reduce | flops 4032 | bytes 16128 | tf_op jit(solution)/shard_map/psum | solution.py:315
  1580.6 17.6 psum.93
  1608.7 293.2 %all-reduce.16.cloned.1.call-done = (bf16[288,6912]{1,0:T(8,128)(2,1)}, bf16[288,3456]{1,0:T(8,128)(2,1)}, bf16[288,1152]{1,0:T(8,128)(2,1)}, bf16[288,4608]{1,0:T(8,128)(2,1)}, bf16[1152,1152]{1,0:T(8,128)(2,1)}) async-done(((bf16[288,6912]{1,0:T(8,128)(2,1)}, bf16[288,3456]{1,0:T(8,128)(2,1)}, bf16[288,1152]{1,0:T(8,128)(2,1)}, bf16[288,4608]{1,0:T(8,128)(2,1)}, bf16[1152,1152]{1,0:T(8,128)(2,1)}), ...) | async-done | bytes 11943952 | tf_op jit(solution)/shard_map/psum | solution.py:314
  (463 shorter events, 431.5 us)
Async XLA Ops:
  7.2 106.2 %all-gather.9.cloned.1.call-start = ((), (), s32[]{:S(2)}) async-start(), calls=%async_computation.7 | async-start | bytes 19906560 | tf_op jit(solution)/shard_map/all_gather | solution.py:71
  8.0 105.5 %copy-start.38 = (bf16[2,1152]{1,0:T(2,128)(2,1)S(1)}, bf16[2,1152]{1,0:T(2,128)(2,1)}, u32[]{:S(2)}) copy-start(bf16[2,1152]{1,0:T(2,128)(2,1)} %param.20) | copy-start | bytes 13828
  8.0 162.9 %all-gather.11.cloned.1.call-start = ((), (), s32[]{:S(2)}) async-start(), calls=%async_computation.8 | async-start | bytes 9953280 | tf_op jit(solution)/shard_map/all_gather | solution.py:73
  8.7 262.8 %all-gather.15.cloned.1.call-start = ((), (), s32[]{:S(2)}) async-start(), calls=%async_computation.10 | async-start | bytes 5898240 | tf_op jit(solution)/shard_map/all_gather | solution.py:118
  25.6 145.3 %copy-start.44 = (f32[2,256]{1,0:T(2,128)}, f32[2,256]{1,0:T(2,128)S(1)}, u32[]{:S(2)}) copy-start(f32[2,256]{1,0:T(2,128)S(1)} %broadcast_multiply_fusion.1) | copy-start | bytes 6148
  26.1 144.8 %copy-start.50 = (f32[2,256]{1,0:T(2,128)}, f32[2,256]{1,0:T(2,128)S(1)}, u32[]{:S(2)}) copy-start(f32[2,256]{1,0:T(2,128)S(1)} %fusion.78) | copy-start | bytes 6148
  182.0 179.4 %all-gather.13.cloned.1.call-start = ((), (), s32[]{:S(2)}) async-start(), calls=%async_computation.9 | async-start | bytes 5898240 | tf_op jit(solution)/shard_map/all_gather | solution.py:117
  184.9 260.5 %all-gather.17.cloned.1.call-start = ((), (), s32[]{:S(2)}) async-start(), calls=%async_computation.11 | async-start | bytes 3317760 | tf_op jit(solution)/shard_map/all_gather | solution.py:75
  185.5 273.8 %all-gather.19.cloned.1.call-start = ((), (), s32[]{:S(2)}) async-start(), calls=%async_computation.12 | async-start | bytes 13271040 | tf_op jit(solution)/shard_map/all_gather | solution.py:77
  186.0 345.8 %all-gather.21.cloned.1.call-start = ((), (), s32[]{:S(2)}) async-start(), calls=%async_computation.13 | async-start | bytes 13271040 | tf_op jit(solution)/shard_map/all_gather | solution.py:79
  186.8 758.4 %reduce-scatter.8.cloned.1.call-start = ((), (), s32[]{:S(2)}) async-start(), calls=%async_computation.14 | async-start | bytes 11796480 | tf_op jit(solution)/shard_map/reduce_scatter | solution.py:234
  782.9 326.9 %reduce-scatter.10.cloned.1.call-start = ((), (), s32[]{:S(2)}) async-start(), calls=%async_computation.15 | async-start | bytes 11796480 | tf_op jit(solution)/shard_map/reduce_scatter | solution.py:235
  793.0 361.1 %reduce-scatter.16.cloned.1.call-start = ((), (), s32[]{:S(2)}) async-start(), calls=%async_computation.18 | async-start | bytes 3317760 | tf_op jit(solution)/shard_map/reduce_scatter | solution.py:294
  797.9 438.5 %reduce-scatter.20.cloned.1.call-start = ((), (), s32[]{:S(2)}) async-start(), calls=%async_computation.20 | async-start | bytes 13271040 | tf_op jit(solution)/shard_map/reduce_scatter | solution.py:306
  812.2 511.9 %reduce-scatter.18.cloned.1.call-start = ((), (), s32[]{:S(2)}) async-start(), calls=%async_computation.19 | async-start | bytes 13271040 | tf_op jit(solution)/shard_map/reduce_scatter | solution.py:300
  823.8 572.3 %reduce-scatter.14.cloned.1.call-start = ((), (), s32[]{:S(2)}) async-start(), calls=%async_computation.17 | async-start | bytes 9953280 | tf_op jit(solution)/shard_map/reduce_scatter | solution.py:288
  824.6 287.7 %copy-start.22 = (bf16[2,256,1152]{2,1,0:T(8,128)(2,1)}, bf16[2,256,1152]{2,1,0:T(8,128)(2,1)S(1)}, u32[]{:S(2)}) copy-start(bf16[2,256,1152]{2,1,0:T(8,128)(2,1)S(1)} %copy.96) | copy-start | bytes 3538948
  947.0 173.6 %copy-start.20 = (bf16[2,256,1152]{2,1,0:T(8,128)(2,1)}, bf16[2,256,1152]{2,1,0:T(8,128)(2,1)S(1)}, u32[]{:S(2)}) copy-start(bf16[2,256,1152]{2,1,0:T(8,128)(2,1)S(1)} %convert_element_type.223) | copy-start | bytes 3538948
  947.0 166.3 %copy-start.1 = (bf16[2,256,1152]{2,1,0:T(8,128)(2,1)S(1)}, bf16[2,256,1152]{2,1,0:T(8,128)(2,1)}, u32[]{:S(2)}) copy-start(bf16[2,256,1152]{2,1,0:T(8,128)(2,1)} %param.19) | copy-start | bytes 3538948
  947.0 166.3 %copy-start.34 = (f32[2,1152]{1,0:T(2,128)S(1)}, f32[2,1152]{1,0:T(2,128)}, u32[]{:S(2)}) copy-start(f32[2,1152]{1,0:T(2,128)} %copy-done.33) | copy-start | bytes 27652
  947.0 166.3 %copy-start.45 = (f32[2,256]{1,0:T(2,128)S(1)}, f32[2,256]{1,0:T(2,128)}, u32[]{:S(2)}) copy-start(f32[2,256]{1,0:T(2,128)} %copy-done.44) | copy-start | bytes 6148
  1120.6 398.1 %reduce-scatter.12.cloned.1.call-start = ((), (), s32[]{:S(2)}) async-start(), calls=%async_computation.16 | async-start | bytes 19906560 | tf_op jit(solution)/shard_map/reduce_scatter | solution.py:282
  1154.0 747.8 %all-reduce.16.cloned.1.call-start = ((), (), s32[]{:S(2)}) async-start(), calls=%async_computation.21 | async-start | bytes 23887872 | tf_op jit(solution)/shard_map/psum | solution.py:314
  1521.8 76.4 %copy-start.40 = (bf16[2,1152]{1,0:T(2,128)(2,1)S(1)}, bf16[2,1152]{1,0:T(2,128)(2,1)}, u32[]{:S(2)}) copy-start(bf16[2,1152]{1,0:T(2,128)(2,1)} %param.20) | copy-start | bytes 13828
  (61 other events, 518.6 us)
Sparse Core Ops, SparseCore 0:
  9.6 103.7 all-gather.8
  115.0 55.8 all-gather.10
  182.1 89.3 all-gather.14
  273.5 87.7 all-gather.12
  362.8 24.1 all-gather.16
  388.4 70.9 all-gather.18
  460.9 70.9 all-gather.20
  783.0 162.1 reduce-scatter.7
  947.6 162.1 reduce-scatter.9
  1112.8 35.6 reduce-scatter.15
  1151.1 85.2 reduce-scatter.19
  1238.8 85.2 reduce-scatter.17
  1327.2 68.8 reduce-scatter.13
  1398.6 120.0 reduce-scatter.11
  1523.7 378.1 all-reduce.15
where the time goes:
time: 1940 us; the launch traced here: 1930 us
  waiting for transfers between devices  1290 us (66%)
  matrix products  325 us (17%)
  blocking collectives  138 us (7%)
  local copies, waits for them, and re-layouts  80.1 us (4%)
  other arithmetic  72.8 us (4%)
  between operations  23.3 us (1%)
    psum x1, waiting for transfers between devices, shards(): lax.psum(owned_modw.astype(jnp.bfloat16), ('rep', 'seq'))  293 us
    reduce_scatter x1, waiting for transfers between devices, shards(): lax.psum_scatter(merge_heads(v_grads), 'seq', scatter_dimension=1, tiled=...  163 us
    reduce_scatter x1, waiting for transfers between devices, shards(): lax.psum_scatter(mod_term.astype(jnp.bfloat16), 'fsdp', scatter_dimension...  123 us
    reduce_scatter x1, waiting for transfers between devices, shards(): lax.psum_scatter(merge_heads(k_grads), 'seq', scatter_dimension=1, tiled=...  121 us
    reduce_scatter x1, waiting for transfers between devices, shards(): lax.psum_scatter(up_wgrad.astype(jnp.bfloat16), 'fsdp', scatter_dimension...  87.7 us
    all_gather x1, waiting for transfers between devices, shards(): lax.all_gather(mod_weight, 'fsdp', axis=0, tiled=True)  86.8 us
    reduce_scatter x1, waiting for transfers between devices, shards(): lax.psum_scatter(down_wgrad.astype(jnp.bfloat16), 'fsdp', scatter_dimensi...  82.3 us
    all_gather x1, waiting for transfers between devices, shards(): lax.all_gather(keys_own, 'seq', axis=1, tiled=True)  77.4 us
  transfers between devices with their start and end apart: 15, of which 13 were waited for; matrix products, arithmetic and copies ran while one was open for 12% of the time, Pallas kernels for 0%

commit v1 on v0

--- a/solution.py
+++ b/solution.py
@@ -7,6 +7,11 @@
 EPS = 1e-06
 GELU_C = 0.7978845608028654
 HIGHEST = lax.Precision.HIGHEST
+
+
+def connect_slot_now(my_tile, lane_axis):
+    right_arr = lax.all_gather(my_tile, lane_axis)
+    return jnp.sum(right_arr, axis=0)
 
 
 def norm_rows(inputs):
@@ -311,7 +316,7 @@
         ).astype(jnp.float32),
     )
     summed = (
-        lax.psum(owned_modw.astype(jnp.bfloat16), ("rep", "seq")).astype(jnp.float32),
+        connect_slot_now(owned_modw.astype(jnp.bfloat16), ("rep", "seq")).astype(jnp.float32),
         lax.psum(owned_modb.astype(jnp.bfloat16), ("rep", "seq")).astype(jnp.float32),
         lax.psum(owned_qkvw.astype(jnp.bfloat16), ("rep", "seq")).astype(jnp.float32),
         lax.psum(owned_qkvb.astype(jnp.bfloat16), ("rep", "seq")).astype(jnp.float32),

time: 1940 us -> 2430 us (1.25)
  waiting for transfers between devices: 1290 us -> 1760 us
    all_gather x0 -> x1, waiting for transfers between devices: none -> 595 us  [connect_slot_now(): right_arr = lax.all_gather(my_tile, lane_axis)]
    psum x1, waiting for transfers between devices: 293 us -> 174 us  [shards(): lax.psum(owned_qkvw.astype(jnp.bfloat16), ('rep', 'seq'))]
  transfers between devices with their start and end apart: 15 -> 16, of which waited for: 13 -> 14; matrix products, arithmetic and copies ran while one was open for 12% -> 10% of each run, Pallas kernels for 0% -> 0%
where the time goes in v1:
time: 2430 us; the launch traced here: 2420 us
  waiting for transfers between devices  1760 us (72%)
  matrix products  325 us (13%)
  blocking collectives  138 us (6%)
  other arithmetic  86.5 us (4%)
  local copies, waits for them, and re-layouts  80.1 us (3%)
    all_gather x1, waiting for transfers between devices, connect_slot_now(): right_arr = lax.all_gather(my_tile, lane_axis)  595 us
    psum x1, waiting for transfers between devices, shards(): lax.psum(owned_qkvw.astype(jnp.bfloat16), ('rep', 'seq'))  174 us
    reduce_scatter x1, waiting for transfers between devices, shards(): lax.psum_scatter(merge_heads(v_grads), 'seq', scatter_dimension=1, tiled=...  163 us
    reduce_scatter x1, waiting for transfers between devices, shards(): lax.psum_scatter(mod_term.astype(jnp.bfloat16), 'fsdp', scatter_dimension...  122 us
    reduce_scatter x1, waiting for transfers between devices, shards(): lax.psum_scatter(merge_heads(k_grads), 'seq', scatter_dimension=1, tiled=...  121 us
    reduce_scatter x1, waiting for transfers between devices, shards(): lax.psum_scatter(up_wgrad.astype(jnp.bfloat16), 'fsdp', scatter_dimension...  87.7 us
    all_gather x1, waiting for transfers between devices, shards(): lax.all_gather(mod_weight, 'fsdp', axis=0, tiled=True)  86.8 us
    reduce_scatter x1, waiting for transfers between devices, shards(): lax.psum_scatter(down_wgrad.astype(jnp.bfloat16), 'fsdp', scatter_dimensi...  82.2 us
  transfers between devices with their start and end apart: 16, of which 14 were waited for; matrix products, arithmetic and copies ran while one was open for 10% of the time, Pallas kernels for 0%

profile of v1, /device:TPU:0, one launch (start us, length us, event | category | flops | bytes accessed | tf_op | source)
XLA Modules:
  0.0 2416.8 jit_solution(16451416415060393768)
XLA Ops:
  12.4 12.9 all-reduce.13
  26.7 86.8 %all-gather.11.cloned.1.call-done = bf16[1152,6912]{1,0:T(8,128)(2,1)} async-done(((bf16[288,6912]{1,0:T(8,128)(2,1)}), bf16[1152,6912]{1,0:T(8,128)(2,1)}) %all-gather.11.cloned.1.call-update) | async-done | bytes 15925264 | tf_op jit(solution)/shard_map/all_gather | solution.py:76
  121.8 49.1 %all-gather.13.cloned.1.call-done = bf16[1152,3456]{1,0:T(8,128)(2,1)} async-done(((bf16[288,3456]{1,0:T(8,128)(2,1)}), bf16[1152,3456]{1,0:T(8,128)(2,1)}) %all-gather.13.cloned.1.call-update) | async-done | bytes 7962640 | tf_op jit(solution)/shard_map/all_gather | solution.py:78
  208.5 63.0 %all-gather.17.cloned.1.call-done = bf16[2,1024,1152]{2,1,0:T(8,128)(2,1)} async-done(((bf16[2,256,1152]{2,1,0:T(8,128)(2,1)}), bf16[2,1024,1152]{2,1,0:T(8,128)(2,1)}) %all-gather.17.cloned.1.call-update) | async-done | bytes 4718608 | tf_op jit(solution)/shard_map/all_gather | solution.py:123
  284.0 77.4 %all-gather.15.cloned.1.call-done = bf16[2,1024,1152]{2,1,0:T(8,128)(2,1)} async-done(((bf16[2,256,1152]{2,1,0:T(8,128)(2,1)}), bf16[2,1024,1152]{2,1,0:T(8,128)(2,1)}) %all-gather.15.cloned.1.call-update) | async-done | bytes 4718608 | tf_op jit(solution)/shard_map/all_gather | solution.py:122
  373.8 71.5 %while.26 = (s32[]{:T(128)}, bf16[16,2,256,72]{2,3,0,1:T(8,128)(2,1)S(1)}, f32[16,2,256]{2,1,0:T(2,128)}, pred[2,1,1024]{2,0,1:T(4,128)(4,1)S(1)}, bf16[16,2,256...) while((s32[]{:T(128)}, ...), condition=%wide.region_5.6_spmd, body=%wide.region_2.5_spmd.sunk | while | flops 157285888 | bytes 7129185 | solution.py:155
  472.1 59.7 %all-gather.23.cloned.1.call-done = bf16[4608,1152]{1,0:T(8,128)(2,1)} async-done(((bf16[1152,1152]{1,0:T(8,128)(2,1)}), bf16[4608,1152]{1,0:T(8,128)(2,1)}) %all-gather.23.cloned.1.call-update) | async-done | bytes 10616848 | tf_op jit(solution)/shard_map/all_gather | solution.py:84
  531.8 13.2 convolution_add_fusion.1
  547.8 39.5 %all-reduce.9 = (f32[]{:T(128)}, f32[]{:T(128)}) all-reduce(f32[]{:T(128)} %get-tuple-element.232, f32[]{:T(128)} %convert_reduce_fusion.2), channel_id=1, replica_groups=mesh['rep'=2,'fsdp'=4,'seq'=4] {'rep','fsdp','seq'}, use_global_device_ids=true, to_apply=%region_9.10 | all-reduce | flops 2 | bytes 16 | tf_op jit(solution)/shard_map/psum | solution.py:330
  591.4 18.8 fusion.87
  630.5 142.3 %while.27 = (s32[]{:T(128)}, bf16[16,2,256,72]{2,3,0,1:T(8,128)(2,1)S(1)}, f32[16,2,1024,72]{2,3,0,1:T(8,128)}, f32[16,2,1024,72]{2,3,0,1:T(8,128)}, pred[2,1,10...) while((s32[]{:T(128)}, ...), condition=%wide.region_16.17_spmd, body=%wide.region_14.16_spmd.sunk | while | flops 382389760 | bytes 18398340 | solution.py:235
  799.1 13.0 convolution_convert_fusion.1
  824.6 120.7 %reduce-scatter.8.cloned.1.call-done = f32[2,256,1152]{2,1,0:T(8,128)} async-done(((f32[2,1024,1152]{2,1,0:T(8,128)}), f32[2,256,1152]{2,1,0:T(8,128)}) %reduce-scatter.8.cloned.1.call-update) | async-done | bytes 2359312 | tf_op jit(solution)/shard_map/reduce_scatter | solution.py:239
  947.1 162.7 %reduce-scatter.10.cloned.1.call-done = f32[2,256,1152]{2,1,0:T(8,128)} async-done(((f32[2,1024,1152]{2,1,0:T(8,128)}), f32[2,256,1152]{2,1,0:T(8,128)}) %reduce-scatter.10.cloned.1.call-update) | async-done | bytes 2359312 | tf_op jit(solution)/shard_map/reduce_scatter | solution.py:240
  1138.5 15.5 convolution_convert_fusion
  1154.1 82.2 %reduce-scatter.20.cloned.1.call-done = bf16[1152,1152]{1,0:T(8,128)(2,1)} async-done(((bf16[4608,1152]{1,0:T(8,128)(2,1)}), bf16[1152,1152]{1,0:T(8,128)(2,1)}) %reduce-scatter.20.cloned.1.call-update) | async-done | bytes 2654224 | tf_op jit(solution)/shard_map/reduce_scatter | solution.py:311
  1236.3 87.7 %reduce-scatter.18.cloned.1.call-done = bf16[288,4608]{1,0:T(8,128)(2,1)} async-done(((bf16[1152,4608]{1,0:T(8,128)(2,1)}), bf16[288,4608]{1,0:T(8,128)(2,1)}) %reduce-scatter.18.cloned.1.call-update) | async-done | bytes 2654224 | tf_op jit(solution)/shard_map/reduce_scatter | solution.py:305
  1324.1 72.1 %reduce-scatter.14.cloned.1.call-done = bf16[288,3456]{1,0:T(8,128)(2,1)} async-done(((bf16[1152,3456]{1,0:T(8,128)(2,1)}), bf16[288,3456]{1,0:T(8,128)(2,1)}) %reduce-scatter.14.cloned.1.call-update) | async-done | bytes 1990672 | tf_op jit(solution)/shard_map/reduce_scatter | solution.py:293
  1396.2 122.5 %reduce-scatter.12.cloned.1.call-done = bf16[288,6912]{1,0:T(8,128)(2,1)} async-done(((bf16[1152,6912]{1,0:T(8,128)(2,1)}), bf16[288,6912]{1,0:T(8,128)(2,1)}) %reduce-scatter.12.cloned.1.call-update) | async-done | bytes 3981328 | tf_op jit(solution)/shard_map/reduce_scatter | solution.py:287
  1537.4 40.0 %all-reduce.10 = (bf16[1728]{0:T(1024)(128)(2,1)S(1)}, bf16[576]{0:T(1024)(128)(2,1)S(1)}, bf16[288]{0:T(512)(128)(2,1)S(1)}, bf16[1152]{0:T(1024)(128)(2,1)S(1)}, bf16[288]{0:T(512)(128)(2,1)S(1)}) all-reduce(bf16[1728]{0:T(1024)(128)(2,1)S(1)} %dynamic-slice.5, ...), channel_id=1, replica_groups=mesh['rep'=2,'fsdp'=4,'seq'=4] {'rep','seq'}, use_global_device_ids=true, to_apply=%region_32.33 | all-reduce | flops 4032 | bytes 16128 | tf_op jit(solution)/shard_map/psum | solution.py:320
  1580.4 17.7 psum.86
  1608.6 174.3 %all-reduce.16.cloned.1.call-done = (bf16[288,3456]{1,0:T(8,128)(2,1)}, bf16[288,1152]{1,0:T(8,128)(2,1)}, bf16[288,4608]{1,0:T(8,128)(2,1)}, bf16[1152,1152]{1,0:T(8,128)(2,1)}) async-done(((bf16[288,3456]{1,0:T(8,128)(2,1)}, bf16[288,1152]{1,0:T(8,128)(2,1)}, bf16[288,4608]{1,0:T(8,128)(2,1)}, bf16[1152,1152]{1,0:T(8,128)(2,1)}), (bf16[288,3456]{1,0:T(8,128)(2,1)}, bf16[288,1152]{1,0:T(8,128)(2,1)}, ...) | async-done | bytes 7962640 | tf_op jit(solution)/shard_map/psum | solution.py:321
  1794.3 594.9 %all-gather.25.cloned.1.call-done = bf16[2304,6912]{1,0:T(8,128)(2,1)} async-done(((bf16[288,6912]{1,0:T(8,128)(2,1)}), bf16[2304,6912]{1,0:T(8,128)(2,1)}) %all-gather.25.cloned.1.call-update) | async-done | bytes 31850512 | tf_op jit(solution)/shard_map/all_gather | solution.py:13
  2389.2 13.6 reduce_sum.287
  (467 shorter events, 455.9 us)
Async XLA Ops:
  7.2 106.2 %all-gather.11.cloned.1.call-start = ((), (), s32[]{:S(2)}) async-start(), calls=%async_computation.7 | async-start | bytes 19906560 | tf_op jit(solution)/shard_map/all_gather | solution.py:76
  8.0 162.9 %all-gather.13.cloned.1.call-start = ((), (), s32[]{:S(2)}) async-start(), calls=%async_computation.8 | async-start | bytes 9953280 | tf_op jit(solution)/shard_map/all_gather | solution.py:78
  8.7 262.8 %all-gather.17.cloned.1.call-start = ((), (), s32[]{:S(2)}) async-start(), calls=%async_computation.10 | async-start | bytes 5898240 | tf_op jit(solution)/shard_map/all_gather | solution.py:123
  25.6 145.3 %copy-start.44 = (f32[2,256]{1,0:T(2,128)}, f32[2,256]{1,0:T(2,128)S(1)}, u32[]{:S(2)}) copy-start(f32[2,256]{1,0:T(2,128)S(1)} %broadcast_multiply_fusion.1) | copy-start | bytes 6148
  26.1 144.8 %copy-start.50 = (f32[2,256]{1,0:T(2,128)}, f32[2,256]{1,0:T(2,128)S(1)}, u32[]{:S(2)}) copy-start(f32[2,256]{1,0:T(2,128)S(1)} %fusion.78) | copy-start | bytes 6148
  182.0 179.4 %all-gather.15.cloned.1.call-start = ((), (), s32[]{:S(2)}) async-start(), calls=%async_computation.9 | async-start | bytes 5898240 | tf_op jit(solution)/shard_map/all_gather | solution.py:122
  184.9 260.5 %all-gather.19.cloned.1.call-start = ((), (), s32[]{:S(2)}) async-start(), calls=%async_computation.11 | async-start | bytes 3317760 | tf_op jit(solution)/shard_map/all_gather | solution.py:80
  185.5 273.8 %all-gather.21.cloned.1.call-start = ((), (), s32[]{:S(2)}) async-start(), calls=%async_computation.12 | async-start | bytes 13271040 | tf_op jit(solution)/shard_map/all_gather | solution.py:82
  186.0 345.8 %all-gather.23.cloned.1.call-start = ((), (), s32[]{:S(2)}) async-start(), calls=%async_computation.13 | async-start | bytes 13271040 | tf_op jit(solution)/shard_map/all_gather | solution.py:84
  186.8 758.4 %reduce-scatter.8.cloned.1.call-start = ((), (), s32[]{:S(2)}) async-start(), calls=%async_computation.14 | async-start | bytes 11796480 | tf_op jit(solution)/shard_map/reduce_scatter | solution.py:239
  782.9 326.9 %reduce-scatter.10.cloned.1.call-start = ((), (), s32[]{:S(2)}) async-start(), calls=%async_computation.15 | async-start | bytes 11796480 | tf_op jit(solution)/shard_map/reduce_scatter | solution.py:240
  793.0 361.1 %reduce-scatter.16.cloned.1.call-start = ((), (), s32[]{:S(2)}) async-start(), calls=%async_computation.18 | async-start | bytes 3317760 | tf_op jit(solution)/shard_map/reduce_scatter | solution.py:299
  797.8 438.5 %reduce-scatter.20.cloned.1.call-start = ((), (), s32[]{:S(2)}) async-start(), calls=%async_computation.20 | async-start | bytes 13271040 | tf_op jit(solution)/shard_map/reduce_scatter | solution.py:311
  812.1 511.9 %reduce-scatter.18.cloned.1.call-start = ((), (), s32[]{:S(2)}) async-start(), calls=%async_computation.19 | async-start | bytes 13271040 | tf_op jit(solution)/shard_map/reduce_scatter | solution.py:305
  823.8 572.4 %reduce-scatter.14.cloned.1.call-start = ((), (), s32[]{:S(2)}) async-start(), calls=%async_computation.17 | async-start | bytes 9953280 | tf_op jit(solution)/shard_map/reduce_scatter | solution.py:293
  824.5 287.7 %copy-start.22 = (bf16[2,256,1152]{2,1,0:T(8,128)(2,1)}, bf16[2,256,1152]{2,1,0:T(8,128)(2,1)S(1)}, u32[]{:S(2)}) copy-start(bf16[2,256,1152]{2,1,0:T(8,128)(2,1)S(1)} %copy.96) | copy-start | bytes 3538948
  947.0 173.6 %copy-start.20 = (bf16[2,256,1152]{2,1,0:T(8,128)(2,1)}, bf16[2,256,1152]{2,1,0:T(8,128)(2,1)S(1)}, u32[]{:S(2)}) copy-start(bf16[2,256,1152]{2,1,0:T(8,128)(2,1)S(1)} %convert_element_type.225) | copy-start | bytes 3538948
  947.0 166.3 %copy-start.1 = (bf16[2,256,1152]{2,1,0:T(8,128)(2,1)S(1)}, bf16[2,256,1152]{2,1,0:T(8,128)(2,1)}, u32[]{:S(2)}) copy-start(bf16[2,256,1152]{2,1,0:T(8,128)(2,1)} %param.19) | copy-start | bytes 3538948
  947.1 166.2 %copy-start.34 = (f32[2,1152]{1,0:T(2,128)S(1)}, f32[2,1152]{1,0:T(2,128)}, u32[]{:S(2)}) copy-start(f32[2,1152]{1,0:T(2,128)} %copy-done.33) | copy-start | bytes 27652
  947.1 166.2 %copy-start.45 = (f32[2,256]{1,0:T(2,128)S(1)}, f32[2,256]{1,0:T(2,128)}, u32[]{:S(2)}) copy-start(f32[2,256]{1,0:T(2,128)} %copy-done.44) | copy-start | bytes 6148
  1120.6 398.1 %reduce-scatter.12.cloned.1.call-start = ((), (), s32[]{:S(2)}) async-start(), calls=%async_computation.16 | async-start | bytes 19906560 | tf_op jit(solution)/shard_map/reduce_scatter | solution.py:287
  1154.0 628.9 %all-reduce.16.cloned.1.call-start = ((), (), s32[]{:S(2)}) async-start(), calls=%async_computation.22 | async-start | bytes 15925248 | tf_op jit(solution)/shard_map/psum | solution.py:321
  1396.2 125.3 %copy-start.2 = (f32[2,256,1152]{2,1,0:T(8,128)S(1)}, f32[2,256,1152]{2,1,0:T(8,128)}, u32[]{:S(2)}) copy-start(f32[2,256,1152]{2,1,0:T(8,128)} %get-tuple-element.233) | copy-start | bytes 7077892
  1396.2 993.0 %all-gather.25.cloned.1.call-start = ((), (), s32[]{:S(2)}) async-start(), calls=%async_computation.21 | async-start | bytes 35831808 | tf_op jit(solution)/shard_map/all_gather | solution.py:13
  (62 other events, 693.8 us)
Sparse Core Ops, SparseCore 0:
  9.6 103.7 all-gather.10
  115.0 55.8 all-gather.12
  182.1 89.3 all-gather.16
  273.5 87.7 all-gather.14
  362.8 24.1 all-gather.18
  388.4 70.9 all-gather.20
  460.9 70.9 all-gather.22
  783.0 162.2 reduce-scatter.7
  947.6 162.1 reduce-scatter.9
  1112.8 35.7 reduce-scatter.15
  1151.1 85.1 reduce-scatter.19
  1238.8 85.2 reduce-scatter.17
  1327.2 68.8 reduce-scatter.13
  1398.6 120.0 reduce-scatter.11
  1523.0 259.9 all-reduce.15
  1784.3 604.7 all-gather.24
